TPU v7x, 1024 devices: a whole 4x4x32 slice. The times are simulated.
1024 devices in a mesh: gx: 8 (over z_hi, core), gy: 4 (over x), gz: 32 (over z_lo, y).
Axes of the slice: x: 4, y: 4, z: 32 (z_hi: 4, z_lo: 8; z = z_hi * 8 + z_lo), core: 2. Of those that a mesh axis runs over, the one named last changes fastest.
Arguments:
- euler_state: float32 [5, 32, 32, 4096], P(None, 'gx', 'gy', 'gz'), as said below
- gravity_state: float32 [4, 32, 32, 4096], P(None, 'gx', 'gy', 'gz'), may hold values from -6 to 6
Outputs:
- section_rate: float32 [5, 32, 32, 4096], P(None, 'gx', 'gy', 'gz')
- gravity_next: float32 [4, 32, 32, 4096], P(None, 'gx', 'gy', 'gz')
- gravity_source: float32 [4, 32, 32, 4096], P(None, 'gx', 'gy', 'gz')
- residual_norm: float32 [], replicated
Inputs may be any that keep to these rules, and one draw needn't show every extreme that they name: `euler_state`: each node's density lies between 0.7 and 3.9 and its pressure, for a ratio of specific heats of 1.4, between 0.7 and 71.
All inputs are finite; a program needn't handle non-finite values.
Results may differ from a plain program's by a relative error of at most 0.0003.
Values sent between devices are 32-bit elements; how exact they have to be, the bound alone decides.
No kernel may reach another device: no remote copies, remote signals or barrier semaphores. Data moves between devices by JAX's collectives and lax.ppermute only.
A program may use at most 32 MiB of HBM per device.

v0:
```python
import functools
import math

import jax
import jax.numpy as jnp
import numpy as np
from jax import lax
from jax.experimental import pallas as pl
from jax.experimental.pallas import tpu as pltpu
from jax.sharding import Mesh
from jax.sharding import PartitionSpec as P


ITERS = 3
GX = ("gx_0", "gx_1")
GZ = ("gz_0", "gz_1")

gamma_gas = 1.4
elem_width = 1.0
cfl_euler = 0.5
alpha_most = 0.5
indicator_level = 0.5 * 10.0 ** (-1.8 * 4.0**0.25)
indicator_slope = math.log((1.0 - 0.0001) / 0.0001) / indicator_level
coupling = 10.0
pseudo_step = 0.3 * elem_width / 7.0
rho_offset = 2.3

NX, NY, NZ = (4, 8, 128)
F32 = jnp.float32


def lgl_tables():
    points = np.array([-1.0, -1.0 / math.sqrt(5.0), 1.0 / math.sqrt(5.0), 1.0])
    weights = np.array([1.0, 5.0, 5.0, 1.0]) / 6.0
    barycentric = np.array(
        [1.0 / np.prod([points[a] - points[b] for b in range(4) if b != a]) for a in range(4)]
    )
    derivative = np.zeros((4, 4))
    for a in range(4):
        for b in range(4):
            if b != a:
                derivative[a, b] = barycentric[b] / barycentric[a] / (points[a] - points[b])
        derivative[a, a] = -np.sum(derivative[a])
    legendre = np.stack(
        [np.ones(4), points, 0.5 * (3.0 * points**2 - 1.0), 0.5 * (5.0 * points**3 - 3.0 * points)],
        axis=1,
    )
    legendre = legendre * np.sqrt((2.0 * np.arange(4) + 1.0) / 2.0)
    gram = np.sum(weights[:, None] * legendre * legendre, axis=0)
    modal_map = (legendre * weights[:, None]).T / gram[:, None]
    return (weights, derivative, modal_map)


WEIGHTS, DERIV, MODAL = lgl_tables()


class Line:
    def __init__(self, dim):
        self.dim = dim
        self.length = (NY, NZ)[dim]
        self.at = lax.broadcasted_iota(jnp.int32, (NY, NZ), dim)
        self.node = self.at % 4
        self.lowest = self.at == 0
        self.highest = self.at == self.length - 1
        self.is0 = self.node == 0
        self.is3 = self.node == 3

    def by_node(self, values):
        v = [float(item) for item in values]
        if v[1] == v[2] and v[0] == v[3]:
            return jnp.where(self.is0 | self.is3, v[0], v[1]).astype(F32)
        return jnp.where(
            self.node < 2,
            jnp.where(self.is0, v[0], v[1]),
            jnp.where(self.is3, v[3], v[2]),
        ).astype(F32)

    def roll(self, value, by):
        return pltpu.roll(value, by % self.length, self.dim)

    def cyc(self, value, k):
        return jnp.where(self.node < 4 - k, self.roll(value, -k), self.roll(value, 4 - k))

    def coef(self, matrix, k, scale=1.0):
        return self.by_node([scale * matrix[i, (i + k) % 4] for i in range(4)])

    def element_sum(self, value):
        value = value + self.cyc(value, 2)
        return value + self.cyc(value, 1)


def load(ref):
    return [[ref[c, x] for x in range(NX)] for c in range(ref.shape[0])]


def pack(comps, flags_ref, outs):
    even = [flags_ref[d] == 0 for d in range(3)]
    xo, zo, yo, yp, zp, xp = outs
    lane = lax.broadcasted_iota(jnp.int32, (NY, NZ), 1)
    first = jnp.zeros((NY, NZ), F32)
    last = jnp.zeros((NY, NZ), F32)
    for c, comp in enumerate(comps):
        xp[c] = jnp.where(even[0], comp[NX - 1], comp[0])
        xo[c] = jnp.where(even[0], comp[0], comp[NX - 1])
        for x in range(NX):
            low, high = (comp[x][0:1, :], comp[x][NY - 1 : NY, :])
            yp[c, pl.ds(x, 1), :] = jnp.where(even[1], high, low)
            yo[c, pl.ds(x, 1), :] = jnp.where(even[1], low, high)
            k = c * NX + x
            here = lane == k
            first = jnp.where(here, pltpu.roll(comp[x], k, 1) if k else comp[x], first)
            last = jnp.where(here, pltpu.roll(comp[x], k + 1, 1), last)
    zp[...] = jnp.where(even[2], last, first)
    zo[...] = jnp.where(even[2], first, last)


class Halo:
    def __init__(self, flags_ref, refs):
        self.even = [flags_ref[d] == 0 for d in range(3)]
        self.refs = refs
        zo, zp = (refs[1][...], refs[4][...])
        self.zlo = jnp.where(self.even[2], zo, zp)
        self.zhi = jnp.where(self.even[2], zp, zo)

    def x_low(self, c):
        return jnp.where(self.even[0], self.refs[0][c], self.refs[5][c])

    def x_high(self, c):
        return jnp.where(self.even[0], self.refs[5][c], self.refs[0][c])

    def row(self, c, x, pair, other):
        line = jnp.where(self.even[1], self.refs[pair][c, pl.ds(x, 1), :], self.refs[other][c, pl.ds(x, 1), :])
        return jnp.broadcast_to(line, (NY, NZ))

    def low(self, dim, c, x):
        if dim == 0:
            return self.row(c, x, 2, 3)
        k = c * NX + x
        return pltpu.roll(self.zlo, (NZ - k) % NZ, 1) if k else self.zlo

    def high(self, dim, c, x):
        if dim == 0:
            return self.row(c, x, 3, 2)
        k = c * NX + x
        return pltpu.roll(self.zhi, NZ - 1 - k, 1)


def message_shapes(n):
    plane, rows, columns = (shape(n, NY, NZ), shape(n, NX, NZ), shape(NY, NZ))
    return [plane, columns, rows, rows, columns, plane]


def log_mean(left, right):
    total = left + right
    gap = right - left
    slope = gap / total
    ratio_sq = slope * slope
    is_close = ratio_sq < 0.0001
    series = 2.0 + ratio_sq * (2.0 / 3.0 + ratio_sq * (2.0 / 5.0 + ratio_sq * (2.0 / 7.0)))
    top = jnp.where(is_close, total, gap)
    low = jnp.where(is_close, series, jnp.log(right / left))
    return top / low


def two_point(left, right, d):
    rho_mean = log_mean(left[0], right[0])
    inv_mean = left[4] * right[4] / log_mean(left[0] * right[4], right[0] * left[4])
    vel = [0.5 * (left[1 + i] + right[1 + i]) for i in range(3)]
    product = left[1] * right[1] + left[2] * right[2] + left[3] * right[3]
    mass = rho_mean * vel[d]
    flux = [mass] + [mass * vel[i] for i in range(3)]
    flux[1 + d] = flux[1 + d] + 0.5 * (left[4] + right[4])
    energy = mass * (0.5 * product + inv_mean * (1.0 / (gamma_gas - 1.0))) + 0.5 * (
        left[4] * right[1 + d] + right[4] * left[1 + d]
    )
    return flux + [energy]


def primitive(u):
    inv = 1.0 / u[0]
    vel = [u[1 + i] * inv for i in range(3)]
    kinetic = u[1] * vel[0] + u[2] * vel[1] + u[3] * vel[2]
    pressure = (gamma_gas - 1.0) * (u[4] - 0.5 * kinetic)
    return (vel, pressure, jnp.sqrt(gamma_gas * pressure * inv))


def face_data(u, d, known=None):
    vel, pressure, sound = known or primitive(u)
    normal = vel[d]
    flux = [u[1 + d]] + [u[1 + i] * normal for i in range(3)] + [(u[4] + pressure) * normal]
    flux[1 + d] = flux[1 + d] + pressure
    return (u, flux, jnp.abs(normal) + sound)


def interface(left, right):
    speed = jnp.maximum(left[2], right[2])
    return [
        0.5 * ((left[1][c] + right[1][c]) - speed * (right[0][c] - left[0][c])) for c in range(5)
    ]


def volume_kernel(u_ref, vol_ref, alpha_ref, fast_ref):
    y, z = (Line(0), Line(1))
    u = load(u_ref)
    known = [primitive([u[c][x] for c in range(5)]) for x in range(NX)]
    nodes = [[u[0][x]] + known[x][0] + [known[x][1]] for x in range(NX)]
    speed = [
        jnp.abs(known[x][0][0]) + jnp.abs(known[x][0][1]) + jnp.abs(known[x][0][2]) + 3.0 * known[x][2]
        for x in range(NX)
    ]
    fast_ref[...] = jnp.maximum(jnp.maximum(speed[0], speed[1]), jnp.maximum(speed[2], speed[3]))

    product = [u[0][x] * known[x][1] for x in range(NX)]
    coeffs = [sum(float(MODAL[a, i]) * product[i] for i in range(4)) for a in range(4)]
    for line in (y, z):
        modal = [line.coef(MODAL, k) for k in range(4)]
        coeffs = [
            modal[0] * value + sum(modal[k] * line.cyc(value, k) for k in range(1, 4))
            for value in coeffs
        ]
    energy = [value * value for value in coeffs]
    total = (energy[0] + energy[1]) + (energy[2] + energy[3])
    low = (energy[0] + energy[1]) + energy[2]
    high = energy[3] + jnp.where(y.is3 | z.is3, low, 0.0)
    share = z.element_sum(y.element_sum(high)) / z.element_sum(y.element_sum(total))
    alpha = alpha_most / (1.0 + jnp.exp(-indicator_slope * (share - indicator_level)))
    alpha_ref[...] = alpha

    volume = [[None] * NX for _ in range(5)]
    for i in range(NX):
        for j in range(i + 1, NX):
            flux = two_point(nodes[i], nodes[j], 0)
            for c in range(5):
                for at, other in ((i, j), (j, i)):
                    term = (2.0 * DERIV[at, other]).astype(np.float32) * flux[c]
                    volume[c][at] = term if volume[c][at] is None else volume[c][at] + term
    for d, line in ((1, y), (2, z)):
        up, across, down = [line.coef(DERIV, k, 2.0) for k in (1, 2, 3)]
        for x in range(NX):
            near = two_point(nodes[x], [line.cyc(a, 1) for a in nodes[x]], d)
            far = two_point(nodes[x], [line.cyc(a, 2) for a in nodes[x]], d)
            for c in range(5):
                volume[c][x] = volume[c][x] + (
                    up * near[c] + down * line.cyc(near[c], 3) + across * far[c]
                )
    keep = 1.0 - alpha
    for c in range(5):
        for x in range(NX):
            vol_ref[c, x] = keep * volume[c][x]


def gravity_parts(field, halo, base, y, z):
    total = [[0.0] * NX for _ in range(4)]
    have = [c for c in range(4) if field[c] is not None]
    where = {c: base + i for i, c in enumerate(have)}

    for c, partner in ((0, 1), (1, 0)):
        if field[partner] is not None:
            for i in range(NX):
                terms = [float(2.0 * DERIV[i, j]) * field[partner][j] for j in range(NX) if DERIV[i, j] != 0.0]
                total[c][i] = total[c][i] + sum(terms[1:], terms[0])
    jumps = {}
    for c in have:
        jumps[c] = (halo.x_low(where[c]) - field[c][0], halo.x_high(where[c]) - field[c][NX - 1])
        for side, x in ((0, 0), (1, NX - 1)):
            total[c][x] = total[c][x] + 6.0 * jumps[c][side]
    for c, partner in ((0, 1), (1, 0)):
        if partner in jumps:
            total[c][0] = total[c][0] - 6.0 * jumps[partner][0]
            total[c][NX - 1] = total[c][NX - 1] + 6.0 * jumps[partner][1]
    for d, line in ((1, y), (2, z)):
        comp = 1 + d
        diag = line.coef(DERIV, 0, 2.0)
        coefs = [line.coef(DERIV, k, 2.0) for k in range(1, 4)]
        sign = line.by_node([-6.0, 0.0, 0.0, 6.0])
        for x in range(NX):
            for c, partner in ((0, comp), (comp, 0)):
                if field[partner] is not None:
                    value = field[partner][x]
                    term = diag * value
                    for k in range(1, 4):
                        term = term + coefs[k - 1] * line.cyc(value, k)
                    total[c][x] = total[c][x] + term
            gaps = {}
            for c in have:
                value = field[c][x]
                prev = jnp.where(line.lowest, halo.low(line.dim, where[c], x), line.roll(value, 1))
                after = jnp.where(line.highest, halo.high(line.dim, where[c], x), line.roll(value, -1))
                beside = jnp.where(line.is0, prev, jnp.where(line.is3, after, value))
                gaps[c] = beside - value
                total[c][x] = total[c][x] + 6.0 * gaps[c]
            for c, partner in ((0, comp), (comp, 0)):
                if partner in gaps:
                    total[c][x] = total[c][x] + sign * gaps[partner]
    return total


def advance(field, halo, base, y, z, source):
    total = gravity_parts(field, halo, base, y, z)
    phi_rate = [total[0][x] - coupling * source[x] for x in range(NX)]
    new = [[None] * NX for _ in range(4)]
    for x in range(NX):
        change = pseudo_step * phi_rate[x]
        new[0][x] = change if field[0] is None else field[0][x] + change
        for c in range(1, 4):
            if field[c] is None:
                new[c][x] = pseudo_step * total[c][x]
            else:
                new[c][x] = field[c][x] + pseudo_step * (total[c][x] - field[c][x])
    return (new, phi_rate)


def pack_kernel(flags_ref, u_ref, g_ref, *outs):
    pack(load(u_ref) + load(g_ref), flags_ref, outs)


def face_kernel(flags_ref, u_ref, g_ref, vol_ref, alpha_ref, *refs):
    halo = Halo(flags_ref, refs[:6])
    rate_ref, field_ref = refs[6:8]
    outs = refs[8:]
    y, z = (Line(0), Line(1))
    u = load(u_ref)
    g = load(g_ref)
    alpha = alpha_ref[...]
    keep = 1.0 - alpha
    known = [primitive([u[c][x] for c in range(5)]) for x in range(NX)]
    total = load(vol_ref)

    own = [face_data([u[c][x] for c in range(5)], 0, known[x]) for x in range(NX)]
    below = face_data([halo.x_low(c) for c in range(5)], 0)
    above = face_data([halo.x_high(c) for c in range(5)], 0)
    chain = [below] + own + [above]
    faces = [interface(chain[i], chain[i + 1]) for i in range(NX + 1)]
    for x in range(NX):
        inner = alpha * float(1.0 / WEIGHTS[x])
        edge = inner + keep * 6.0
        low_coef = edge if x == 0 else inner
        high_coef = edge if x == NX - 1 else inner
        for c in range(5):
            total[c][x] = total[c][x] + (high_coef * faces[x + 1][c] - low_coef * faces[x][c])
    for d, line in ((1, y), (2, z)):
        inner = alpha * line.by_node(1.0 / WEIGHTS)
        low_coef = inner + keep * line.by_node([6.0, 0.0, 0.0, 0.0])
        high_coef = inner + keep * line.by_node([0.0, 0.0, 0.0, 6.0])
        for x in range(NX):
            mine = face_data([u[c][x] for c in range(5)], d, known[x])
            prev = face_data(
                [
                    jnp.where(line.lowest, halo.low(line.dim, c, x), line.roll(u[c][x], 1))
                    for c in range(5)
                ],
                d,
            )
            after = face_data(
                [jnp.where(line.highest, halo.high(line.dim, c, x), u[c][x]) for c in range(5)], d
            )
            face = interface(prev, mine)
            end = interface(mine, after)
            for c in range(5):
                following = jnp.where(line.highest, end[c], line.roll(face[c], -1))
                total[c][x] = total[c][x] + (high_coef * following - low_coef * face[c])
    rate = [[-2.0 * total[c][x] for x in range(NX)] for c in range(5)]
    for x in range(NX):
        for i in range(3):
            rate[1 + i][x] = rate[1 + i][x] - u[0][x] * g[1 + i][x]
        rate[4][x] = rate[4][x] - (
            u[1][x] * g[1][x] + u[2][x] * g[2][x] + u[3][x] * g[3][x]
        )
        for c in range(5):
            rate_ref[c, x] = rate[c][x]

    source = [u[0][x] - rho_offset for x in range(NX)]
    new, _ = advance(g, halo, 5, y, z, source)
    slope = [(-pseudo_step * coupling) * rate[0][x] for x in range(NX)]
    comps = new + [slope]
    for c in range(5):
        for x in range(NX):
            field_ref[c, x] = comps[c][x]
    pack(comps, flags_ref, outs)


def middle_kernel(flags_ref, u_ref, rate_ref, field_ref, *refs):
    halo = Halo(flags_ref, refs[:6])
    next_ref = refs[6]
    outs = refs[7:]
    y, z = (Line(0), Line(1))
    field = load(field_ref)
    new, _ = advance(field[:4], halo, 0, y, z, [u_ref[0, x] - rho_offset for x in range(NX)])
    slope, _ = advance([field[4], None, None, None], halo, 4, y, z, [rate_ref[0, x] for x in range(NX)])
    comps = new + slope
    for c in range(8):
        for x in range(NX):
            next_ref[c, x] = comps[c][x]
    pack(comps, flags_ref, outs)


def last_kernel(flags_ref, u_ref, rate_ref, field_ref, fast_ref, *refs):
    halo = Halo(flags_ref, refs[:6])
    next_ref, stat_ref = refs[6:]
    y, z = (Line(0), Line(1))
    field = load(field_ref)
    source = [u_ref[0, x] - rho_offset for x in range(NX)]
    new, base_rate = advance(field[:4], halo, 0, y, z, source)
    slope, slope_rate = advance(field[4:], halo, 4, y, z, [rate_ref[0, x] for x in range(NX)])
    comps = new + slope
    for c in range(8):
        for x in range(NX):
            next_ref[c, x] = comps[c][x]
    weight = y.by_node(WEIGHTS) * z.by_node(WEIGHTS)

    def total(values):
        by_x = [float(WEIGHTS[x]) * values[x] for x in range(NX)]
        return jnp.sum(((by_x[0] + by_x[1]) + (by_x[2] + by_x[3])) * weight)

    stats = [
        jnp.max(fast_ref[...]),
        total([a * a for a in base_rate]),
        total([a * b for a, b in zip(base_rate, slope_rate)]),
        total([b * b for b in slope_rate]),
        total(base_rate),
        total(slope_rate),
        total(source),
    ]
    lane = lax.broadcasted_iota(jnp.int32, (1, NZ), 1)
    out = jnp.zeros((1, NZ), F32)
    for i, value in enumerate(stats):
        out = jnp.where(lane == i, value, out)
    stat_ref[...] = out


def finish_kernel(weight_total, u_ref, rate_ref, field_ref, stat_ref, grav_ref, source_ref, norm_ref):
    stat = stat_ref[...]
    part = [stat[:, i : i + 1] for i in range(7)]
    step = cfl_euler * elem_width / (7.0 * part[0])
    mean = part[6] * (1.0 / weight_total)
    shift = coupling * mean
    squares = (
        part[1]
        + step * (2.0 * part[2] + step * part[3])
        + shift * (2.0 * (part[4] + step * part[5]) + shift * weight_total)
    )
    norm_ref[...] = jnp.sqrt(jnp.maximum(squares, 0.0) * (1.0 / weight_total))
    raised = (ITERS * pseudo_step) * shift
    for x in range(NX):
        phi = field_ref[0, x] + step * field_ref[4, x] + raised
        grad = [field_ref[c, x] + step * field_ref[4 + c, x] for c in range(1, 4)]
        grav_ref[0, x] = phi
        for c in range(3):
            grav_ref[1 + c, x] = grad[c]
        rho = u_ref[0, x] + step * rate_ref[0, x]
        work = 0.0
        for c in range(3):
            source_ref[c, x] = -rho * grad[c]
            work = work + (u_ref[1 + c, x] + step * rate_ref[1 + c, x]) * grad[c]
        source_ref[3, x] = -work


def call(kernel, out_shape, flops, flags=None):
    def run(*args):
        specs = [pl.BlockSpec(memory_space=pltpu.VMEM)] * len(args)
        args = [pltpu.with_memory_space_constraint(a, pltpu.VMEM) for a in args]
        if flags is not None:
            specs = [pl.BlockSpec(memory_space=pltpu.SMEM)] + specs
            args = [flags] + args
        return pl.pallas_call(
            kernel,
            in_specs=specs,
            out_specs=[pl.BlockSpec(memory_space=pltpu.VMEM)] * len(out_shape),
            out_shape=out_shape,
            cost_estimate=pl.CostEstimate(flops=flops, bytes_accessed=400000, transcendentals=0),
        )(*args)

    return run


def pair_of(i, size):
    return i ^ 1


def other_of(i, size):
    return (i + 1 if i % 2 else i - 1) % size


ROUTES = (
    (GX, other_of),
    (GZ, other_of),
    ("gy", other_of),
    ("gy", pair_of),
    (GZ, pair_of),
    (GX, pair_of),
)


def exchange(messages):
    received = []
    for message, (axis, partner) in zip(messages, ROUTES):
        size = lax.axis_size(axis)
        received.append(lax.ppermute(message, axis, [(a, partner(a, size)) for a in range(size)]))
    return received


def slots(stat, axis):
    size = lax.axis_size(axis)
    row = lax.broadcasted_iota(jnp.int32, (size, NZ), 0)
    lane = lax.broadcasted_iota(jnp.int32, (1, NZ), 1)
    every = lax.psum(jnp.where(row == lax.axis_index(axis), stat, 0.0), axis)
    return jnp.where(
        lane == 0, jnp.max(every, axis=0, keepdims=True), jnp.sum(every, axis=0, keepdims=True)
    )


def spread(stat):
    names = ("gx_0", "gx_1", "gy", "gz_0", "gz_1")
    sizes = [lax.axis_size(name) for name in names]
    ring = sizes[0] * sizes[3]
    pairs = []
    for at in np.ndindex(*sizes):
        a, core, b, c, e = at
        place = (a * sizes[3] + c + core * sizes[4] + e - (sizes[3] // 2 - 1)) % ring
        to = (place // sizes[3], core, b, place % sizes[3], e)
        pairs.append(
            (int(np.ravel_multi_index(at, sizes)), int(np.ravel_multi_index(to, sizes)))
        )
    return lax.ppermute(stat, names, pairs)


def over_all(stat):
    for axis in ("gx_1", "gy", "gz_1"):
        stat = slots(stat, axis)
    stat = spread(stat)
    for axis in ("gx_1", "gz_1", "gx_0"):
        stat = slots(stat, axis)
    return stat


def shape(*dims):
    return pltpu.VMEM(dims, F32)


def local(u, g):
    weight_total = float(
        8.0
        * (u.shape[1] // 4 * lax.axis_size(GX))
        * (u.shape[2] // 4 * lax.axis_size("gy"))
        * (u.shape[3] // 4 * lax.axis_size(GZ))
    )
    full = (NX, NY, NZ)
    flags = jnp.stack([lax.axis_index(axis) & 1 for axis in ("gx_1", "gy", "gz_1")])
    messages = call(pack_kernel, message_shapes(9), 10**5, flags)(u, g)
    received = exchange(messages)
    vol, alpha, fast = call(
        volume_kernel, [shape(5, *full), shape(NY, NZ), shape(NY, NZ)], 10**7
    )(u)
    rate, field, *messages = call(
        face_kernel, [shape(5, *full), shape(5, *full)] + message_shapes(5), 10**6, flags
    )(u, g, vol, alpha, *received)
    received = exchange(messages)
    field, *messages = call(middle_kernel, [shape(8, *full)] + message_shapes(8), 10**6, flags)(
        u, rate, field, *received
    )
    received = exchange(messages)
    field, stat = call(last_kernel, [shape(8, *full), shape(1, NZ)], 10**6, flags)(
        u, rate, field, fast, *received
    )
    stat = over_all(stat)
    gravity, gravity_source, norm = call(
        functools.partial(finish_kernel, weight_total),
        [jax.ShapeDtypeStruct((4, *full), F32)] * 2 + [jax.ShapeDtypeStruct((1, 1), F32)],
        10**5,
    )(u, rate, field, stat)
    return (rate, gravity, gravity_source, norm.reshape(()))


def solution(mesh):
    torus = Mesh(
        mesh.devices.reshape(4, 2, mesh.shape["gy"], 8, 4), ("gx_0", "gx_1", "gy", "gz_0", "gz_1")
    )
    placed = (P(None, GX, "gy", GZ), P(None, GX, "gy", GZ))
    return jax.shard_map(
        local,
        mesh=torus,
        in_specs=placed,
        out_specs=(P(None, GX, "gy", GZ), P(None, GX, "gy", GZ), P(None, GX, "gy", GZ), P()),
        check_vma=False,
    )
```

profile of v0, /device:TPU:8, one launch (start us, length us, event | category | flops | bytes accessed | tf_op | source)
XLA Modules:
  0.0 180.4 jit_solution(14949096263376664292)
XLA Ops:
  0.6 0.6 pad_add_fusion.flags_ref
  1.2 0.0 copy-start
  1.2 0.9 copy-done
  2.1 0.0 copy-start.1
  2.1 0.8 copy-done.1
  3.0 0.8 shard_map.58
  3.8 0.0 copy-start.2
  3.8 22.6 %collective-permute-start = (f32[9,8,128]{2,1,0:T(8,128)S(1)}, f32[9,8,128]{2,1,0:T(8,128)S(1)}, u32[]{:S(2)}, u32[]{:S(2)}) collective-permute-start(f32[9,8,128]{2,1,0:T(8,128)S(1)} %get-tuple-element.35), channel_id=1, source_target_pairs={{0,896},{128,256},{256,128},{384,512},{512,384},{640,768},{768,640... | collective-permute-start | bytes 110600 | tf_op jit(solution)/shard_map/ppermute | solution.py:498
  26.4 1.9 %collective-permute-start.5 = (f32[9,8,128]{2,1,0:T(8,128)S(1)}, f32[9,8,128]{2,1,0:T(8,128)S(1)}, u32[]{:S(2)}, u32[]{:S(2)}) collective-permute-start(f32[9,8,128]{2,1,0:T(8,128)S(1)} %get-tuple-element.40), channel_id=1, source_target_pairs={{0,128},{128,0},{256,384},{384,256},{512,640},{640,512},{768,896},... | collective-permute-start | bytes 110600 | tf_op jit(solution)/shard_map/ppermute | solution.py:498
  28.3 4.7 %collective-permute-start.2 = (f32[9,4,128]{2,1,0:T(4,128)S(1)}, f32[9,4,128]{2,1,0:T(4,128)S(1)}, u32[]{:S(2)}, u32[]{:S(2)}) collective-permute-start(f32[9,4,128]{2,1,0:T(4,128)S(1)} %get-tuple-element.37), channel_id=1, source_target_pairs={{0,96},{32,64},{64,32},{96,0},{1,97},{33,65},{65,33},{97,1},{2,98}... | collective-permute-start | bytes 55304 | tf_op jit(solution)/shard_map/ppermute | solution.py:498
  33.0 2.1 %collective-permute-start.3 = (f32[9,4,128]{2,1,0:T(4,128)S(1)}, f32[9,4,128]{2,1,0:T(4,128)S(1)}, u32[]{:S(2)}, u32[]{:S(2)}) collective-permute-start(f32[9,4,128]{2,1,0:T(4,128)S(1)} %get-tuple-element.38), channel_id=1, source_target_pairs={{0,32},{32,0},{64,96},{96,64},{1,33},{33,1},{65,97},{97,65},{2,34}... | collective-permute-start | bytes 55304 | tf_op jit(solution)/shard_map/ppermute | solution.py:498
  35.1 3.5 %collective-permute-start.1 = (f32[8,128]{1,0:T(8,128)S(1)}, f32[8,128]{1,0:T(8,128)S(1)}, u32[]{:S(2)}, u32[]{:S(2)}) collective-permute-start(f32[8,128]{1,0:T(8,128)S(1)} %get-tuple-element.36), channel_id=1, source_target_pairs={{0,31},{1,2},{2,1},{3,4},{4,3},{5,6},{6,5},{7,8},{8,7},{9,10},{10,... | collective-permute-start | bytes 12296 | tf_op jit(solution)/shard_map/ppermute | solution.py:498
  38.6 2.0 %collective-permute-done.1.refs_1_ = f32[8,128]{1,0:T(8,128)S(1)} collective-permute-done((f32[8,128]{1,0:T(8,128)S(1)}, f32[8,128]{1,0:T(8,128)S(1)}, u32[]{:S(2)}, u32[]{:S(2)}) %collective-permute-start.1) | collective-permute-done | bytes 4128 | tf_op jit(solution)/shard_map/ppermute | solution.py:498
  40.6 11.1 %collective-permute-start.4 = (f32[8,128]{1,0:T(8,128)S(1)}, f32[8,128]{1,0:T(8,128)S(1)}, u32[]{:S(2)}, u32[]{:S(2)}) collective-permute-start(f32[8,128]{1,0:T(8,128)S(1)} %get-tuple-element.39), channel_id=1, source_target_pairs={{0,1},{1,0},{2,3},{3,2},{4,5},{5,4},{6,7},{7,6},{8,9},{9,8},{10,11... | collective-permute-start | bytes 12296 | tf_op jit(solution)/shard_map/ppermute | solution.py:498
  51.7 0.4 shard_map.57
  52.1 1.1 collective-permute-done.4.refs_4_
  53.2 0.0 collective-permute-done.2.refs_2_
  53.2 0.0 collective-permute-done.3.refs_3_
  53.2 0.0 collective-permute-done.refs_0_
  53.2 0.0 collective-permute-done.5.refs_5_
  53.3 0.0 copy-done.2
  53.3 1.2 shard_map.59
  54.5 3.9 %collective-permute-start.10 = (f32[8,128]{1,0:T(8,128)S(1)}, f32[8,128]{1,0:T(8,128)S(1)}, u32[]{:S(2)}, u32[]{:S(2)}) collective-permute-start(f32[8,128]{1,0:T(8,128)S(1)} %get-tuple-element.47), channel_id=1, source_target_pairs={{0,1},{1,0},{2,3},{3,2},{4,5},{5,4},{6,7},{7,6},{8,9},{9,8},{10,11... | collective-permute-start | bytes 12296 | tf_op jit(solution)/shard_map/ppermute | solution.py:498
  58.4 1.9 %collective-permute-start.11 = (f32[5,8,128]{2,1,0:T(8,128)S(1)}, f32[5,8,128]{2,1,0:T(8,128)S(1)}, u32[]{:S(2)}, u32[]{:S(2)}) collective-permute-start(f32[5,8,128]{2,1,0:T(8,128)S(1)} %get-tuple-element.48), channel_id=1, source_target_pairs={{0,128},{128,0},{256,384},{384,256},{512,640},{640,512},{768,896},... | collective-permute-start | bytes 61448 | tf_op jit(solution)/shard_map/ppermute | solution.py:498
  60.3 8.5 %collective-permute-start.6 = (f32[5,8,128]{2,1,0:T(8,128)S(1)}, f32[5,8,128]{2,1,0:T(8,128)S(1)}, u32[]{:S(2)}, u32[]{:S(2)}) collective-permute-start(f32[5,8,128]{2,1,0:T(8,128)S(1)} %get-tuple-element.43), channel_id=1, source_target_pairs={{0,896},{128,256},{256,128},{384,512},{512,384},{640,768},{768,640... | collective-permute-start | bytes 61448 | tf_op jit(solution)/shard_map/ppermute | solution.py:498
  68.9 3.0 %collective-permute-start.8 = (f32[5,4,128]{2,1,0:T(4,128)S(1)}, f32[5,4,128]{2,1,0:T(4,128)S(1)}, u32[]{:S(2)}, u32[]{:S(2)}) collective-permute-start(f32[5,4,128]{2,1,0:T(4,128)S(1)} %get-tuple-element.45), channel_id=1, source_target_pairs={{0,96},{32,64},{64,32},{96,0},{1,97},{33,65},{65,33},{97,1},{2,98}... | collective-permute-start | bytes 30728 | tf_op jit(solution)/shard_map/ppermute | solution.py:498
  71.9 2.6 %collective-permute-start.9 = (f32[5,4,128]{2,1,0:T(4,128)S(1)}, f32[5,4,128]{2,1,0:T(4,128)S(1)}, u32[]{:S(2)}, u32[]{:S(2)}) collective-permute-start(f32[5,4,128]{2,1,0:T(4,128)S(1)} %get-tuple-element.46), channel_id=1, source_target_pairs={{0,32},{32,0},{64,96},{96,64},{1,33},{33,1},{65,97},{97,65},{2,34}... | collective-permute-start | bytes 30728 | tf_op jit(solution)/shard_map/ppermute | solution.py:498
  74.5 0.0 collective-permute-done.10.refs_4_
  74.5 1.9 %collective-permute-start.7 = (f32[8,128]{1,0:T(8,128)S(1)}, f32[8,128]{1,0:T(8,128)S(1)}, u32[]{:S(2)}, u32[]{:S(2)}) collective-permute-start(f32[8,128]{1,0:T(8,128)S(1)} %get-tuple-element.44), channel_id=1, source_target_pairs={{0,31},{1,2},{2,1},{3,4},{4,3},{5,6},{6,5},{7,8},{8,7},{9,10},{10,... | collective-permute-start | bytes 12296 | tf_op jit(solution)/shard_map/ppermute | solution.py:498
  76.5 3.6 %collective-permute-done.7.refs_1_ = f32[8,128]{1,0:T(8,128)S(1)} collective-permute-done((f32[8,128]{1,0:T(8,128)S(1)}, f32[8,128]{1,0:T(8,128)S(1)}, u32[]{:S(2)}, u32[]{:S(2)}) %collective-permute-start.7) | collective-permute-done | bytes 4128 | tf_op jit(solution)/shard_map/ppermute | solution.py:498
  80.0 0.0 collective-permute-done.8.refs_2_
  80.0 0.0 collective-permute-done.9.refs_3_
  80.0 0.0 collective-permute-done.11.refs_5_
  80.1 0.0 collective-permute-done.6.refs_0_
  80.1 1.0 shard_map.60
  81.0 1.9 %collective-permute-start.13 = (f32[8,128]{1,0:T(8,128)S(1)}, f32[8,128]{1,0:T(8,128)S(1)}, u32[]{:S(2)}, u32[]{:S(2)}) collective-permute-start(f32[8,128]{1,0:T(8,128)S(1)} %get-tuple-element.52), channel_id=1, source_target_pairs={{0,31},{1,2},{2,1},{3,4},{4,3},{5,6},{6,5},{7,8},{8,7},{9,10},{10,... | collective-permute-start | bytes 12296 | tf_op jit(solution)/shard_map/ppermute | solution.py:498
  83.0 4.3 %collective-permute-start.12 = (f32[8,8,128]{2,1,0:T(8,128)S(1)}, f32[8,8,128]{2,1,0:T(8,128)S(1)}, u32[]{:S(2)}, u32[]{:S(2)}) collective-permute-start(f32[8,8,128]{2,1,0:T(8,128)S(1)} %get-tuple-element.51), channel_id=1, source_target_pairs={{0,896},{128,256},{256,128},{384,512},{512,384},{640,768},{768,640... | collective-permute-start | bytes 98312 | tf_op jit(solution)/shard_map/ppermute | solution.py:498
  87.3 3.8 %collective-permute-start.17 = (f32[8,8,128]{2,1,0:T(8,128)S(1)}, f32[8,8,128]{2,1,0:T(8,128)S(1)}, u32[]{:S(2)}, u32[]{:S(2)}) collective-permute-start(f32[8,8,128]{2,1,0:T(8,128)S(1)} %get-tuple-element.56), channel_id=1, source_target_pairs={{0,128},{128,0},{256,384},{384,256},{512,640},{640,512},{768,896},... | collective-permute-start | bytes 98312 | tf_op jit(solution)/shard_map/ppermute | solution.py:498
  91.1 4.5 %collective-permute-start.14 = (f32[8,4,128]{2,1,0:T(4,128)S(1)}, f32[8,4,128]{2,1,0:T(4,128)S(1)}, u32[]{:S(2)}, u32[]{:S(2)}) collective-permute-start(f32[8,4,128]{2,1,0:T(4,128)S(1)} %get-tuple-element.53), channel_id=1, source_target_pairs={{0,96},{32,64},{64,32},{96,0},{1,97},{33,65},{65,33},{97,1},{2,98}... | collective-permute-start | bytes 49160 | tf_op jit(solution)/shard_map/ppermute | solution.py:498
  95.7 2.1 %collective-permute-start.15 = (f32[8,4,128]{2,1,0:T(4,128)S(1)}, f32[8,4,128]{2,1,0:T(4,128)S(1)}, u32[]{:S(2)}, u32[]{:S(2)}) collective-permute-start(f32[8,4,128]{2,1,0:T(4,128)S(1)} %get-tuple-element.54), channel_id=1, source_target_pairs={{0,32},{32,0},{64,96},{96,64},{1,33},{33,1},{65,97},{97,65},{2,34}... | collective-permute-start | bytes 49160 | tf_op jit(solution)/shard_map/ppermute | solution.py:498
  97.8 0.0 collective-permute-done.13.refs_1_
  97.8 17.7 %collective-permute-start.16 = (f32[8,128]{1,0:T(8,128)S(1)}, f32[8,128]{1,0:T(8,128)S(1)}, u32[]{:S(2)}, u32[]{:S(2)}) collective-permute-start(f32[8,128]{1,0:T(8,128)S(1)} %get-tuple-element.55), channel_id=1, source_target_pairs={{0,1},{1,0},{2,3},{3,2},{4,5},{5,4},{6,7},{7,6},{8,9},{9,8},{10,11... | collective-permute-start | bytes 12296 | tf_op jit(solution)/shard_map/ppermute | solution.py:498
  115.6 1.6 collective-permute-done.16.refs_4_
  117.1 0.0 collective-permute-done.14.refs_2_
  117.1 0.0 collective-permute-done.15.refs_3_
  117.1 0.0 collective-permute-done.12.refs_0_
  117.1 0.0 collective-permute-done.17.refs_5_
  117.1 1.1 shard_map.61
  118.2 0.1 broadcast_select_fusion.5
  118.3 2.4 %psum.42 = f32[2,128]{1,0:T(2,128)S(1)} all-reduce(f32[2,128]{1,0:T(2,128)S(1)} %broadcast_select_fusion.5), channel_id=1, replica_groups=mesh['gx_0'=4,'gx_1'=2,'gy'=4,'gz_0'=8,'gz_1'=4] {'gx_1'}, use_global_device_ids=true, to_apply=%region_0.1 | all-reduce | flops 256 | bytes 2048 | tf_op jit(solution)/shard_map/psum | solution.py:506
  120.7 0.1 broadcast_select_fusion.3
  120.8 9.5 %psum.43 = f32[4,128]{1,0:T(4,128)S(1)} all-reduce(f32[4,128]{1,0:T(4,128)S(1)} %broadcast_select_fusion.3), channel_id=1, replica_groups=mesh['gx_0'=4,'gx_1'=2,'gy'=4,'gz_0'=8,'gz_1'=4] {'gy'}, use_global_device_ids=true, to_apply=%region_3.4 | all-reduce | flops 512 | bytes 4096 | tf_op jit(solution)/shard_map/psum | solution.py:506
  130.4 0.1 broadcast_select_fusion.2
  130.4 9.7 %psum.44 = f32[4,128]{1,0:T(4,128)S(1)} all-reduce(f32[4,128]{1,0:T(4,128)S(1)} %broadcast_select_fusion.2), channel_id=1, replica_groups=mesh['gx_0'=4,'gx_1'=2,'gy'=4,'gz_0'=8,'gz_1'=4] {'gz_1'}, use_global_device_ids=true, to_apply=%region_6.7 | all-reduce | flops 512 | bytes 4096 | tf_op jit(solution)/shard_map/psum | solution.py:506
  140.2 1.9 %collective-permute-start.18 = (f32[1,128]{1,0:T(1,128)S(1)}, f32[1,128]{1,0:T(1,128)S(1)}, u32[]{:S(2)}, u32[]{:S(2)}) collective-permute-start(f32[1,128]{1,0:T(1,128)S(1)} %compare_select_fusion.1), channel_id=1, source_target_pairs={{0,788},{1,793},{2,798},{3,3},{4,792},{5,797},{6,2},{7,7},{8,796},... | collective-permute-start | bytes 1544 | tf_op jit(solution)/shard_map/ppermute | solution.py:524
  142.1 0.6 copy.6
  142.7 3.8 %collective-permute-done.18 = f32[1,128]{1,0:T(1,128)S(1)} collective-permute-done((f32[1,128]{1,0:T(1,128)S(1)}, f32[1,128]{1,0:T(1,128)S(1)}, u32[]{:S(2)}, u32[]{:S(2)}) %collective-permute-start.18) | collective-permute-done | bytes 544 | tf_op jit(solution)/shard_map/ppermute | solution.py:524
  146.5 0.1 broadcast_select_fusion.4
  146.6 2.4 %psum.45 = f32[2,128]{1,0:T(2,128)S(1)} all-reduce(f32[2,128]{1,0:T(2,128)S(1)} %broadcast_select_fusion.4), channel_id=1, replica_groups=mesh['gx_0'=4,'gx_1'=2,'gy'=4,'gz_0'=8,'gz_1'=4] {'gx_1'}, use_global_device_ids=true, to_apply=%region_9.10 | all-reduce | flops 256 | bytes 2048 | tf_op jit(solution)/shard_map/psum | solution.py:506
  149.1 0.1 broadcast_select_fusion.1
  149.1 8.6 %psum.46 = f32[4,128]{1,0:T(4,128)S(1)} all-reduce(f32[4,128]{1,0:T(4,128)S(1)} %broadcast_select_fusion.1), channel_id=1, replica_groups=mesh['gx_0'=4,'gx_1'=2,'gy'=4,'gz_0'=8,'gz_1'=4] {'gz_1'}, use_global_device_ids=true, to_apply=%region_12.13 | all-reduce | flops 512 | bytes 4096 | tf_op jit(solution)/shard_map/psum | solution.py:506
  157.8 0.1 broadcast_select_fusion
  157.9 21.5 %psum.47 = f32[4,128]{1,0:T(4,128)S(1)} all-reduce(f32[4,128]{1,0:T(4,128)S(1)} %broadcast_select_fusion), channel_id=1, replica_groups=mesh['gx_0'=4,'gx_1'=2,'gy'=4,'gz_0'=8,'gz_1'=4] {'gx_0'}, use_global_device_ids=true, to_apply=%region_15.16 | all-reduce | flops 512 | bytes 4096 | tf_op jit(solution)/shard_map/psum | solution.py:506
  179.4 1.0 shard_map.62
  (16 shorter events, 0.2 us)
Async XLA Ops:
  1.2 0.9 copy-start
  2.1 0.8 copy-start.1
  3.8 49.5 %copy-start.2 = (f32[4,4,8,128]{3,2,1,0:T(8,128)S(1)}, f32[4,4,8,128]{3,2,1,0:T(8,128)}, u32[]{:S(2)}) copy-start(f32[4,4,8,128]{3,2,1,0:T(8,128)} %g_ref.3) | copy-start | bytes 196612
  3.8 49.5 %collective-permute-start = (f32[9,8,128]{2,1,0:T(8,128)S(1)}, f32[9,8,128]{2,1,0:T(8,128)S(1)}, u32[]{:S(2)}, u32[]{:S(2)}) collective-permute-start(f32[9,8,128]{2,1,0:T(8,128)S(1)} %get-tuple-element.35), channel_id=1, source_target_pairs={{0,896},{128,256},{256,128},{384,512},{512,384},{640,768},{768,640... | collective-permute-start | bytes 110600 | tf_op jit(solution)/shard_map/ppermute | solution.py:498
  26.4 26.9 %collective-permute-start.5 = (f32[9,8,128]{2,1,0:T(8,128)S(1)}, f32[9,8,128]{2,1,0:T(8,128)S(1)}, u32[]{:S(2)}, u32[]{:S(2)}) collective-permute-start(f32[9,8,128]{2,1,0:T(8,128)S(1)} %get-tuple-element.40), channel_id=1, source_target_pairs={{0,128},{128,0},{256,384},{384,256},{512,640},{640,512},{768,896},... | collective-permute-start | bytes 110600 | tf_op jit(solution)/shard_map/ppermute | solution.py:498
  28.3 25.0 %collective-permute-start.2 = (f32[9,4,128]{2,1,0:T(4,128)S(1)}, f32[9,4,128]{2,1,0:T(4,128)S(1)}, u32[]{:S(2)}, u32[]{:S(2)}) collective-permute-start(f32[9,4,128]{2,1,0:T(4,128)S(1)} %get-tuple-element.37), channel_id=1, source_target_pairs={{0,96},{32,64},{64,32},{96,0},{1,97},{33,65},{65,33},{97,1},{2,98}... | collective-permute-start | bytes 55304 | tf_op jit(solution)/shard_map/ppermute | solution.py:498
  33.0 20.3 %collective-permute-start.3 = (f32[9,4,128]{2,1,0:T(4,128)S(1)}, f32[9,4,128]{2,1,0:T(4,128)S(1)}, u32[]{:S(2)}, u32[]{:S(2)}) collective-permute-start(f32[9,4,128]{2,1,0:T(4,128)S(1)} %get-tuple-element.38), channel_id=1, source_target_pairs={{0,32},{32,0},{64,96},{96,64},{1,33},{33,1},{65,97},{97,65},{2,34}... | collective-permute-start | bytes 55304 | tf_op jit(solution)/shard_map/ppermute | solution.py:498
  35.1 5.5 %collective-permute-start.1 = (f32[8,128]{1,0:T(8,128)S(1)}, f32[8,128]{1,0:T(8,128)S(1)}, u32[]{:S(2)}, u32[]{:S(2)}) collective-permute-start(f32[8,128]{1,0:T(8,128)S(1)} %get-tuple-element.36), channel_id=1, source_target_pairs={{0,31},{1,2},{2,1},{3,4},{4,3},{5,6},{6,5},{7,8},{8,7},{9,10},{10,... | collective-permute-start | bytes 12296 | tf_op jit(solution)/shard_map/ppermute | solution.py:498
  40.6 12.6 %collective-permute-start.4 = (f32[8,128]{1,0:T(8,128)S(1)}, f32[8,128]{1,0:T(8,128)S(1)}, u32[]{:S(2)}, u32[]{:S(2)}) collective-permute-start(f32[8,128]{1,0:T(8,128)S(1)} %get-tuple-element.39), channel_id=1, source_target_pairs={{0,1},{1,0},{2,3},{3,2},{4,5},{5,4},{6,7},{7,6},{8,9},{9,8},{10,11... | collective-permute-start | bytes 12296 | tf_op jit(solution)/shard_map/ppermute | solution.py:498
  54.5 20.1 %collective-permute-start.10 = (f32[8,128]{1,0:T(8,128)S(1)}, f32[8,128]{1,0:T(8,128)S(1)}, u32[]{:S(2)}, u32[]{:S(2)}) collective-permute-start(f32[8,128]{1,0:T(8,128)S(1)} %get-tuple-element.47), channel_id=1, source_target_pairs={{0,1},{1,0},{2,3},{3,2},{4,5},{5,4},{6,7},{7,6},{8,9},{9,8},{10,11... | collective-permute-start | bytes 12296 | tf_op jit(solution)/shard_map/ppermute | solution.py:498
  58.4 21.7 %collective-permute-start.11 = (f32[5,8,128]{2,1,0:T(8,128)S(1)}, f32[5,8,128]{2,1,0:T(8,128)S(1)}, u32[]{:S(2)}, u32[]{:S(2)}) collective-permute-start(f32[5,8,128]{2,1,0:T(8,128)S(1)} %get-tuple-element.48), channel_id=1, source_target_pairs={{0,128},{128,0},{256,384},{384,256},{512,640},{640,512},{768,896},... | collective-permute-start | bytes 61448 | tf_op jit(solution)/shard_map/ppermute | solution.py:498
  60.3 19.7 %collective-permute-start.6 = (f32[5,8,128]{2,1,0:T(8,128)S(1)}, f32[5,8,128]{2,1,0:T(8,128)S(1)}, u32[]{:S(2)}, u32[]{:S(2)}) collective-permute-start(f32[5,8,128]{2,1,0:T(8,128)S(1)} %get-tuple-element.43), channel_id=1, source_target_pairs={{0,896},{128,256},{256,128},{384,512},{512,384},{640,768},{768,640... | collective-permute-start | bytes 61448 | tf_op jit(solution)/shard_map/ppermute | solution.py:498
  68.9 11.2 %collective-permute-start.8 = (f32[5,4,128]{2,1,0:T(4,128)S(1)}, f32[5,4,128]{2,1,0:T(4,128)S(1)}, u32[]{:S(2)}, u32[]{:S(2)}) collective-permute-start(f32[5,4,128]{2,1,0:T(4,128)S(1)} %get-tuple-element.45), channel_id=1, source_target_pairs={{0,96},{32,64},{64,32},{96,0},{1,97},{33,65},{65,33},{97,1},{2,98}... | collective-permute-start | bytes 30728 | tf_op jit(solution)/shard_map/ppermute | solution.py:498
  71.9 8.1 %collective-permute-start.9 = (f32[5,4,128]{2,1,0:T(4,128)S(1)}, f32[5,4,128]{2,1,0:T(4,128)S(1)}, u32[]{:S(2)}, u32[]{:S(2)}) collective-permute-start(f32[5,4,128]{2,1,0:T(4,128)S(1)} %get-tuple-element.46), channel_id=1, source_target_pairs={{0,32},{32,0},{64,96},{96,64},{1,33},{33,1},{65,97},{97,65},{2,34}... | collective-permute-start | bytes 30728 | tf_op jit(solution)/shard_map/ppermute | solution.py:498
  74.5 5.5 %collective-permute-start.7 = (f32[8,128]{1,0:T(8,128)S(1)}, f32[8,128]{1,0:T(8,128)S(1)}, u32[]{:S(2)}, u32[]{:S(2)}) collective-permute-start(f32[8,128]{1,0:T(8,128)S(1)} %get-tuple-element.44), channel_id=1, source_target_pairs={{0,31},{1,2},{2,1},{3,4},{4,3},{5,6},{6,5},{7,8},{8,7},{9,10},{10,... | collective-permute-start | bytes 12296 | tf_op jit(solution)/shard_map/ppermute | solution.py:498
  81.0 16.8 %collective-permute-start.13 = (f32[8,128]{1,0:T(8,128)S(1)}, f32[8,128]{1,0:T(8,128)S(1)}, u32[]{:S(2)}, u32[]{:S(2)}) collective-permute-start(f32[8,128]{1,0:T(8,128)S(1)} %get-tuple-element.52), channel_id=1, source_target_pairs={{0,31},{1,2},{2,1},{3,4},{4,3},{5,6},{6,5},{7,8},{8,7},{9,10},{10,... | collective-permute-start | bytes 12296 | tf_op jit(solution)/shard_map/ppermute | solution.py:498
  83.0 34.1 %collective-permute-start.12 = (f32[8,8,128]{2,1,0:T(8,128)S(1)}, f32[8,8,128]{2,1,0:T(8,128)S(1)}, u32[]{:S(2)}, u32[]{:S(2)}) collective-permute-start(f32[8,8,128]{2,1,0:T(8,128)S(1)} %get-tuple-element.51), channel_id=1, source_target_pairs={{0,896},{128,256},{256,128},{384,512},{512,384},{640,768},{768,640... | collective-permute-start | bytes 98312 | tf_op jit(solution)/shard_map/ppermute | solution.py:498
  87.3 29.8 %collective-permute-start.17 = (f32[8,8,128]{2,1,0:T(8,128)S(1)}, f32[8,8,128]{2,1,0:T(8,128)S(1)}, u32[]{:S(2)}, u32[]{:S(2)}) collective-permute-start(f32[8,8,128]{2,1,0:T(8,128)S(1)} %get-tuple-element.56), channel_id=1, source_target_pairs={{0,128},{128,0},{256,384},{384,256},{512,640},{640,512},{768,896},... | collective-permute-start | bytes 98312 | tf_op jit(solution)/shard_map/ppermute | solution.py:498
  91.1 26.0 %collective-permute-start.14 = (f32[8,4,128]{2,1,0:T(4,128)S(1)}, f32[8,4,128]{2,1,0:T(4,128)S(1)}, u32[]{:S(2)}, u32[]{:S(2)}) collective-permute-start(f32[8,4,128]{2,1,0:T(4,128)S(1)} %get-tuple-element.53), channel_id=1, source_target_pairs={{0,96},{32,64},{64,32},{96,0},{1,97},{33,65},{65,33},{97,1},{2,98}... | collective-permute-start | bytes 49160 | tf_op jit(solution)/shard_map/ppermute | solution.py:498
  95.7 21.4 %collective-permute-start.15 = (f32[8,4,128]{2,1,0:T(4,128)S(1)}, f32[8,4,128]{2,1,0:T(4,128)S(1)}, u32[]{:S(2)}, u32[]{:S(2)}) collective-permute-start(f32[8,4,128]{2,1,0:T(4,128)S(1)} %get-tuple-element.54), channel_id=1, source_target_pairs={{0,32},{32,0},{64,96},{96,64},{1,33},{33,1},{65,97},{97,65},{2,34}... | collective-permute-start | bytes 49160 | tf_op jit(solution)/shard_map/ppermute | solution.py:498
  97.8 19.3 %collective-permute-start.16 = (f32[8,128]{1,0:T(8,128)S(1)}, f32[8,128]{1,0:T(8,128)S(1)}, u32[]{:S(2)}, u32[]{:S(2)}) collective-permute-start(f32[8,128]{1,0:T(8,128)S(1)} %get-tuple-element.55), channel_id=1, source_target_pairs={{0,1},{1,0},{2,3},{3,2},{4,5},{5,4},{6,7},{7,6},{8,9},{9,8},{10,11... | collective-permute-start | bytes 12296 | tf_op jit(solution)/shard_map/ppermute | solution.py:498
  140.2 6.4 %collective-permute-start.18 = (f32[1,128]{1,0:T(1,128)S(1)}, f32[1,128]{1,0:T(1,128)S(1)}, u32[]{:S(2)}, u32[]{:S(2)}) collective-permute-start(f32[1,128]{1,0:T(1,128)S(1)} %compare_select_fusion.1), channel_id=1, source_target_pairs={{0,788},{1,793},{2,798},{3,3},{4,792},{5,797},{6,2},{7,7},{8,796},... | collective-permute-start | bytes 1544 | tf_op jit(solution)/shard_map/ppermute | solution.py:524
where the time goes:
time: 181 us; the launch traced here: 180 us
  starting transfers between devices  104 us (57%)
  blocking collectives  54.2 us (30%)
  waiting for transfers between devices  12.1 us (7%)
  Pallas kernels  5.42 us (3%)
  local copies, waits for them, and re-layouts  2.37 us (1%)
    ppermute x18, starting transfers between devices, exchange(): lax.ppermute(message, axis, [(a, partner(a, size)) for a in range(size)])  102 us
    psum x6, blocking collectives, slots(): every = lax.psum(jnp.where(row == lax.axis_index(axis), stat, 0.0), axis)  54.2 us
    ppermute x18, waiting for transfers between devices, exchange(): lax.ppermute(message, axis, [(a, partner(a, size)) for a in range(size)])  8.28 us
    pallas_call x6, Pallas kernels, run(): pl.pallas_call(kernel, in_specs=specs, out_specs=[pl.BlockSpec(memory_spa...  5.42 us
    ppermute x1, waiting for transfers between devices, spread(): return lax.ppermute(stat, names, pairs)  3.78 us
  transfers between devices with their start and end apart: 19, of which 5 were waited for; matrix products, arithmetic and copies ran while one was open for 0% of the time, Pallas kernels for 0%

commit v1 on v0

--- a/solution.py
+++ b/solution.py
@@ -93,8 +93,12 @@
     return [[ref[c, x] for x in range(NX)] for c in range(ref.shape[0])]
 
 
-def pack(comps, flags_ref, outs):
-    even = [flags_ref[d] == 0 for d in range(3)]
+def is_even():
+    return [lax.axis_index(axis) % 2 == 0 for axis in ("gx_1", "gy", "gz_1")]
+
+
+def pack(comps, outs):
+    even = is_even()
     xo, zo, yo, yp, zp, xp = outs
     lane = lax.broadcasted_iota(jnp.int32, (NY, NZ), 1)
     first = jnp.zeros((NY, NZ), F32)
@@ -115,8 +119,8 @@
 
 
 class Halo:
-    def __init__(self, flags_ref, refs):
-        self.even = [flags_ref[d] == 0 for d in range(3)]
+    def __init__(self, refs):
+        self.even = is_even()
         self.refs = refs
         zo, zp = (refs[1][...], refs[4][...])
         self.zlo = jnp.where(self.even[2], zo, zp)
@@ -310,12 +314,14 @@
     return (new, phi_rate)
 
 
-def pack_kernel(flags_ref, u_ref, g_ref, *outs):
-    pack(load(u_ref) + load(g_ref), flags_ref, outs)
-
-
-def face_kernel(flags_ref, u_ref, g_ref, vol_ref, alpha_ref, *refs):
-    halo = Halo(flags_ref, refs[:6])
+def pack_kernel(u_ref, g_ref, u_out, g_out, *outs):
+    u_out[...] = u_ref[...]
+    g_out[...] = g_ref[...]
+    pack(load(u_ref) + load(g_ref), outs)
+
+
+def face_kernel(u_ref, g_ref, vol_ref, alpha_ref, *refs):
+    halo = Halo(refs[:6])
     rate_ref, field_ref = refs[6:8]
     outs = refs[8:]
     y, z = (Line(0), Line(1))
@@ -376,11 +382,11 @@
     for c in range(5):
         for x in range(NX):
             field_ref[c, x] = comps[c][x]
-    pack(comps, flags_ref, outs)
-
-
-def middle_kernel(flags_ref, u_ref, rate_ref, field_ref, *refs):
-    halo = Halo(flags_ref, refs[:6])
+    pack(comps, outs)
+
+
+def middle_kernel(u_ref, rate_ref, field_ref, *refs):
+    halo = Halo(refs[:6])
     next_ref = refs[6]
     outs = refs[7:]
     y, z = (Line(0), Line(1))
@@ -391,11 +397,11 @@
     for c in range(8):
         for x in range(NX):
             next_ref[c, x] = comps[c][x]
-    pack(comps, flags_ref, outs)
-
-
-def last_kernel(flags_ref, u_ref, rate_ref, field_ref, fast_ref, *refs):
-    halo = Halo(flags_ref, refs[:6])
+    pack(comps, outs)
+
+
+def last_kernel(u_ref, rate_ref, field_ref, fast_ref, *refs):
+    halo = Halo(refs[:6])
     next_ref, stat_ref = refs[6:]
     y, z = (Line(0), Line(1))
     field = load(field_ref)
@@ -455,16 +461,13 @@
         source_ref[3, x] = -work
 
 
-def call(kernel, out_shape, flops, flags=None):
+def call(kernel, out_shape, flops, on_chip=True):
     def run(*args):
-        specs = [pl.BlockSpec(memory_space=pltpu.VMEM)] * len(args)
-        args = [pltpu.with_memory_space_constraint(a, pltpu.VMEM) for a in args]
-        if flags is not None:
-            specs = [pl.BlockSpec(memory_space=pltpu.SMEM)] + specs
-            args = [flags] + args
+        if on_chip:
+            args = [pltpu.with_memory_space_constraint(a, pltpu.VMEM) for a in args]
         return pl.pallas_call(
             kernel,
-            in_specs=specs,
+            in_specs=[pl.BlockSpec(memory_space=pltpu.VMEM)] * len(args),
             out_specs=[pl.BlockSpec(memory_space=pltpu.VMEM)] * len(out_shape),
             out_shape=out_shape,
             cost_estimate=pl.CostEstimate(flops=flops, bytes_accessed=400000, transcendentals=0),
@@ -499,11 +502,9 @@
     return received
 
 
-def slots(stat, axis):
-    size = lax.axis_size(axis)
-    row = lax.broadcasted_iota(jnp.int32, (size, NZ), 0)
+def gather(stat, axis):
     lane = lax.broadcasted_iota(jnp.int32, (1, NZ), 1)
-    every = lax.psum(jnp.where(row == lax.axis_index(axis), stat, 0.0), axis)
+    every = lax.all_gather(stat, axis, tiled=True)
     return jnp.where(
         lane == 0, jnp.max(every, axis=0, keepdims=True), jnp.sum(every, axis=0, keepdims=True)
     )
@@ -526,10 +527,10 @@
 
 def over_all(stat):
     for axis in ("gx_1", "gy", "gz_1"):
-        stat = slots(stat, axis)
+        stat = gather(stat, axis)
     stat = spread(stat)
     for axis in ("gx_1", "gz_1", "gx_0"):
-        stat = slots(stat, axis)
+        stat = gather(stat, axis)
     return stat
 
 
@@ -545,21 +546,22 @@
         * (u.shape[3] // 4 * lax.axis_size(GZ))
     )
     full = (NX, NY, NZ)
-    flags = jnp.stack([lax.axis_index(axis) & 1 for axis in ("gx_1", "gy", "gz_1")])
-    messages = call(pack_kernel, message_shapes(9), 10**5, flags)(u, g)
+    u, g, *messages = call(
+        pack_kernel, [shape(5, *full), shape(4, *full)] + message_shapes(9), 10**5, False
+    )(u, g)
     received = exchange(messages)
     vol, alpha, fast = call(
         volume_kernel, [shape(5, *full), shape(NY, NZ), shape(NY, NZ)], 10**7
     )(u)
     rate, field, *messages = call(
-        face_kernel, [shape(5, *full), shape(5, *full)] + message_shapes(5), 10**6, flags
+        face_kernel, [shape(5, *full), shape(5, *full)] + message_shapes(5), 10**6
     )(u, g, vol, alpha, *received)
     received = exchange(messages)
-    field, *messages = call(middle_kernel, [shape(8, *full)] + message_shapes(8), 10**6, flags)(
+    field, *messages = call(middle_kernel, [shape(8, *full)] + message_shapes(8), 10**6)(
         u, rate, field, *received
     )
     received = exchange(messages)
-    field, stat = call(last_kernel, [shape(8, *full), shape(1, NZ)], 10**6, flags)(
+    field, stat = call(last_kernel, [shape(8, *full), shape(1, NZ)], 10**6)(
         u, rate, field, fast, *received
     )
     stat = over_all(stat)

time: 181 us -> 182 us (level)
  waiting for transfers between devices: 12.1 us -> 17.2 us
  starting transfers between devices: 104 us -> 108 us
  blocking collectives: 54.2 us -> 51 us
    psum x6 -> x0, blocking collectives: 54.2 us -> none  [slots(): every = lax.psum(jnp.where(row == lax.axis_index(axis), stat, 0.0), axis)]
    all_gather x0 -> x6, blocking collectives: none -> 51 us  [gather(): every = lax.all_gather(stat, axis, tiled=True)]
    ppermute x18, waiting for transfers between devices: 8.28 us -> 13.4 us  [exchange(): lax.ppermute(message, axis, [(a, partner(a, size)) for a in range(size)])]
    ppermute x18, starting transfers between devices: 102 us -> 106 us  [exchange(): lax.ppermute(message, axis, [(a, partner(a, size)) for a in range(size)])]
  transfers between devices with their start and end apart: 19 -> 19, of which waited for: 5 -> 7; matrix products, arithmetic and copies ran while one was open for 0% -> 0% of each run, Pallas kernels for 0% -> 0%
where the time goes in v1:
time: 182 us; the launch traced here: 181 us
  starting transfers between devices  108 us (59%)
  blocking collectives  51 us (28%)
  waiting for transfers between devices  17.2 us (9%)
  Pallas kernels  3.66 us (2%)
    ppermute x18, starting transfers between devices, exchange(): lax.ppermute(message, axis, [(a, partner(a, size)) for a in range(size)])  106 us
    all_gather x6, blocking collectives, gather(): every = lax.all_gather(stat, axis, tiled=True)  51 us
    ppermute x18, waiting for transfers between devices, exchange(): lax.ppermute(message, axis, [(a, partner(a, size)) for a in range(size)])  13.4 us
    ppermute x1, waiting for transfers between devices, spread(): return lax.ppermute(stat, names, pairs)  3.79 us
    pallas_call x6, Pallas kernels, run(): pl.pallas_call(kernel, in_specs=[pl.BlockSpec(memory_space=pltpu.VMEM)] *...  3.66 us
  transfers between devices with their start and end apart: 19, of which 7 were waited for; matrix products, arithmetic and copies ran while one was open for 0% of the time, Pallas kernels for 0%

profile of v1, /device:TPU:8, one launch (start us, length us, event | category | flops | bytes accessed | tf_op | source)
XLA Modules:
  0.0 181.3 jit_solution(15072432382332197481)
XLA Ops:
  0.6 1.0 shard_map.57
  1.7 22.4 %collective-permute-start = (f32[9,8,128]{2,1,0:T(8,128)S(1)}, f32[9,8,128]{2,1,0:T(8,128)S(1)}, u32[]{:S(2)}, u32[]{:S(2)}) collective-permute-start(f32[9,8,128]{2,1,0:T(8,128)S(1)} %get-tuple-element.39), channel_id=1, source_target_pairs={{0,896},{128,256},{256,128},{384,512},{512,384},{640,768},{768,640... | collective-permute-start | bytes 110600 | tf_op jit(solution)/shard_map/ppermute | solution.py:501
  24.1 1.9 %collective-permute-start.5 = (f32[9,8,128]{2,1,0:T(8,128)S(1)}, f32[9,8,128]{2,1,0:T(8,128)S(1)}, u32[]{:S(2)}, u32[]{:S(2)}) collective-permute-start(f32[9,8,128]{2,1,0:T(8,128)S(1)} %get-tuple-element.44), channel_id=1, source_target_pairs={{0,128},{128,0},{256,384},{384,256},{512,640},{640,512},{768,896},... | collective-permute-start | bytes 110600 | tf_op jit(solution)/shard_map/ppermute | solution.py:501
  26.0 4.7 %collective-permute-start.2 = (f32[9,4,128]{2,1,0:T(4,128)S(1)}, f32[9,4,128]{2,1,0:T(4,128)S(1)}, u32[]{:S(2)}, u32[]{:S(2)}) collective-permute-start(f32[9,4,128]{2,1,0:T(4,128)S(1)} %get-tuple-element.41), channel_id=1, source_target_pairs={{0,96},{32,64},{64,32},{96,0},{1,97},{33,65},{65,33},{97,1},{2,98}... | collective-permute-start | bytes 55304 | tf_op jit(solution)/shard_map/ppermute | solution.py:501
  30.7 2.1 %collective-permute-start.3 = (f32[9,4,128]{2,1,0:T(4,128)S(1)}, f32[9,4,128]{2,1,0:T(4,128)S(1)}, u32[]{:S(2)}, u32[]{:S(2)}) collective-permute-start(f32[9,4,128]{2,1,0:T(4,128)S(1)} %get-tuple-element.42), channel_id=1, source_target_pairs={{0,32},{32,0},{64,96},{96,64},{1,33},{33,1},{65,97},{97,65},{2,34}... | collective-permute-start | bytes 55304 | tf_op jit(solution)/shard_map/ppermute | solution.py:501
  32.9 3.5 %collective-permute-start.1 = (f32[8,128]{1,0:T(8,128)S(1)}, f32[8,128]{1,0:T(8,128)S(1)}, u32[]{:S(2)}, u32[]{:S(2)}) collective-permute-start(f32[8,128]{1,0:T(8,128)S(1)} %get-tuple-element.40), channel_id=1, source_target_pairs={{0,31},{1,2},{2,1},{3,4},{4,3},{5,6},{6,5},{7,8},{8,7},{9,10},{10,... | collective-permute-start | bytes 12296 | tf_op jit(solution)/shard_map/ppermute | solution.py:501
  36.4 2.0 %collective-permute-done.1.refs_1_ = f32[8,128]{1,0:T(8,128)S(1)} collective-permute-done((f32[8,128]{1,0:T(8,128)S(1)}, f32[8,128]{1,0:T(8,128)S(1)}, u32[]{:S(2)}, u32[]{:S(2)}) %collective-permute-start.1) | collective-permute-done | bytes 4128 | tf_op jit(solution)/shard_map/ppermute | solution.py:501
  38.4 11.1 %collective-permute-start.4 = (f32[8,128]{1,0:T(8,128)S(1)}, f32[8,128]{1,0:T(8,128)S(1)}, u32[]{:S(2)}, u32[]{:S(2)}) collective-permute-start(f32[8,128]{1,0:T(8,128)S(1)} %get-tuple-element.43), channel_id=1, source_target_pairs={{0,1},{1,0},{2,3},{3,2},{4,5},{5,4},{6,7},{7,6},{8,9},{9,8},{10,11... | collective-permute-start | bytes 12296 | tf_op jit(solution)/shard_map/ppermute | solution.py:501
  49.4 0.4 shard_map.58
  49.9 1.1 collective-permute-done.4.refs_4_
  51.0 0.0 collective-permute-done.2.refs_2_
  51.0 0.0 collective-permute-done.3.refs_3_
  51.0 0.0 collective-permute-done.refs_0_
  51.0 0.0 collective-permute-done.5.refs_5_
  51.0 0.5 shard_map.59
  51.6 1.9 %collective-permute-start.11 = (f32[5,8,128]{2,1,0:T(8,128)S(1)}, f32[5,8,128]{2,1,0:T(8,128)S(1)}, u32[]{:S(2)}, u32[]{:S(2)}) collective-permute-start(f32[5,8,128]{2,1,0:T(8,128)S(1)} %get-tuple-element.52), channel_id=1, source_target_pairs={{0,128},{128,0},{256,384},{384,256},{512,640},{640,512},{768,896},... | collective-permute-start | bytes 61448 | tf_op jit(solution)/shard_map/ppermute | solution.py:501
  53.5 8.5 %collective-permute-start.6 = (f32[5,8,128]{2,1,0:T(8,128)S(1)}, f32[5,8,128]{2,1,0:T(8,128)S(1)}, u32[]{:S(2)}, u32[]{:S(2)}) collective-permute-start(f32[5,8,128]{2,1,0:T(8,128)S(1)} %get-tuple-element.47), channel_id=1, source_target_pairs={{0,896},{128,256},{256,128},{384,512},{512,384},{640,768},{768,640... | collective-permute-start | bytes 61448 | tf_op jit(solution)/shard_map/ppermute | solution.py:501
  62.0 3.0 %collective-permute-start.8 = (f32[5,4,128]{2,1,0:T(4,128)S(1)}, f32[5,4,128]{2,1,0:T(4,128)S(1)}, u32[]{:S(2)}, u32[]{:S(2)}) collective-permute-start(f32[5,4,128]{2,1,0:T(4,128)S(1)} %get-tuple-element.49), channel_id=1, source_target_pairs={{0,96},{32,64},{64,32},{96,0},{1,97},{33,65},{65,33},{97,1},{2,98}... | collective-permute-start | bytes 30728 | tf_op jit(solution)/shard_map/ppermute | solution.py:501
  65.1 2.6 %collective-permute-start.9 = (f32[5,4,128]{2,1,0:T(4,128)S(1)}, f32[5,4,128]{2,1,0:T(4,128)S(1)}, u32[]{:S(2)}, u32[]{:S(2)}) collective-permute-start(f32[5,4,128]{2,1,0:T(4,128)S(1)} %get-tuple-element.50), channel_id=1, source_target_pairs={{0,32},{32,0},{64,96},{96,64},{1,33},{33,1},{65,97},{97,65},{2,34}... | collective-permute-start | bytes 30728 | tf_op jit(solution)/shard_map/ppermute | solution.py:501
  67.7 3.9 %collective-permute-start.10 = (f32[8,128]{1,0:T(8,128)S(1)}, f32[8,128]{1,0:T(8,128)S(1)}, u32[]{:S(2)}, u32[]{:S(2)}) collective-permute-start(f32[8,128]{1,0:T(8,128)S(1)} %get-tuple-element.51), channel_id=1, source_target_pairs={{0,1},{1,0},{2,3},{3,2},{4,5},{5,4},{6,7},{7,6},{8,9},{9,8},{10,11... | collective-permute-start | bytes 12296 | tf_op jit(solution)/shard_map/ppermute | solution.py:501
  71.6 1.6 collective-permute-done.10.refs_4_
  73.2 1.9 %collective-permute-start.7 = (f32[8,128]{1,0:T(8,128)S(1)}, f32[8,128]{1,0:T(8,128)S(1)}, u32[]{:S(2)}, u32[]{:S(2)}) collective-permute-start(f32[8,128]{1,0:T(8,128)S(1)} %get-tuple-element.48), channel_id=1, source_target_pairs={{0,31},{1,2},{2,1},{3,4},{4,3},{5,6},{6,5},{7,8},{8,7},{9,10},{10,... | collective-permute-start | bytes 12296 | tf_op jit(solution)/shard_map/ppermute | solution.py:501
  75.1 3.6 %collective-permute-done.7.refs_1_ = f32[8,128]{1,0:T(8,128)S(1)} collective-permute-done((f32[8,128]{1,0:T(8,128)S(1)}, f32[8,128]{1,0:T(8,128)S(1)}, u32[]{:S(2)}, u32[]{:S(2)}) %collective-permute-start.7) | collective-permute-done | bytes 4128 | tf_op jit(solution)/shard_map/ppermute | solution.py:501
  78.7 0.0 collective-permute-done.8.refs_2_
  78.7 0.0 collective-permute-done.9.refs_3_
  78.7 0.0 collective-permute-done.11.refs_5_
  78.7 0.0 collective-permute-done.6.refs_0_
  78.7 0.3 shard_map.60
  79.0 3.4 %collective-permute-start.12 = (f32[8,8,128]{2,1,0:T(8,128)S(1)}, f32[8,8,128]{2,1,0:T(8,128)S(1)}, u32[]{:S(2)}, u32[]{:S(2)}) collective-permute-start(f32[8,8,128]{2,1,0:T(8,128)S(1)} %get-tuple-element.55), channel_id=1, source_target_pairs={{0,896},{128,256},{256,128},{384,512},{512,384},{640,768},{768,640... | collective-permute-start | bytes 98312 | tf_op jit(solution)/shard_map/ppermute | solution.py:501
  82.5 4.7 %collective-permute-start.17 = (f32[8,8,128]{2,1,0:T(8,128)S(1)}, f32[8,8,128]{2,1,0:T(8,128)S(1)}, u32[]{:S(2)}, u32[]{:S(2)}) collective-permute-start(f32[8,8,128]{2,1,0:T(8,128)S(1)} %get-tuple-element.60), channel_id=1, source_target_pairs={{0,128},{128,0},{256,384},{384,256},{512,640},{640,512},{768,896},... | collective-permute-start | bytes 98312 | tf_op jit(solution)/shard_map/ppermute | solution.py:501
  87.2 4.5 %collective-permute-start.14 = (f32[8,4,128]{2,1,0:T(4,128)S(1)}, f32[8,4,128]{2,1,0:T(4,128)S(1)}, u32[]{:S(2)}, u32[]{:S(2)}) collective-permute-start(f32[8,4,128]{2,1,0:T(4,128)S(1)} %get-tuple-element.57), channel_id=1, source_target_pairs={{0,96},{32,64},{64,32},{96,0},{1,97},{33,65},{65,33},{97,1},{2,98}... | collective-permute-start | bytes 49160 | tf_op jit(solution)/shard_map/ppermute | solution.py:501
  91.7 2.1 %collective-permute-start.15 = (f32[8,4,128]{2,1,0:T(4,128)S(1)}, f32[8,4,128]{2,1,0:T(4,128)S(1)}, u32[]{:S(2)}, u32[]{:S(2)}) collective-permute-start(f32[8,4,128]{2,1,0:T(4,128)S(1)} %get-tuple-element.58), channel_id=1, source_target_pairs={{0,32},{32,0},{64,96},{96,64},{1,33},{33,1},{65,97},{97,65},{2,34}... | collective-permute-start | bytes 49160 | tf_op jit(solution)/shard_map/ppermute | solution.py:501
  93.8 1.9 %collective-permute-start.13 = (f32[8,128]{1,0:T(8,128)S(1)}, f32[8,128]{1,0:T(8,128)S(1)}, u32[]{:S(2)}, u32[]{:S(2)}) collective-permute-start(f32[8,128]{1,0:T(8,128)S(1)} %get-tuple-element.56), channel_id=1, source_target_pairs={{0,31},{1,2},{2,1},{3,4},{4,3},{5,6},{6,5},{7,8},{8,7},{9,10},{10,... | collective-permute-start | bytes 12296 | tf_op jit(solution)/shard_map/ppermute | solution.py:501
  95.8 3.6 %collective-permute-done.13.refs_1_ = f32[8,128]{1,0:T(8,128)S(1)} collective-permute-done((f32[8,128]{1,0:T(8,128)S(1)}, f32[8,128]{1,0:T(8,128)S(1)}, u32[]{:S(2)}, u32[]{:S(2)}) %collective-permute-start.13) | collective-permute-done | bytes 4128 | tf_op jit(solution)/shard_map/ppermute | solution.py:501
  99.3 21.4 %collective-permute-start.16 = (f32[8,128]{1,0:T(8,128)S(1)}, f32[8,128]{1,0:T(8,128)S(1)}, u32[]{:S(2)}, u32[]{:S(2)}) collective-permute-start(f32[8,128]{1,0:T(8,128)S(1)} %get-tuple-element.59), channel_id=1, source_target_pairs={{0,1},{1,0},{2,3},{3,2},{4,5},{5,4},{6,7},{7,6},{8,9},{9,8},{10,11... | collective-permute-start | bytes 12296 | tf_op jit(solution)/shard_map/ppermute | solution.py:501
  120.8 1.6 collective-permute-done.16.refs_4_
  122.4 0.0 collective-permute-done.14.refs_2_
  122.4 0.0 collective-permute-done.15.refs_3_
  122.4 0.0 collective-permute-done.12.refs_0_
  122.4 0.0 collective-permute-done.17.refs_5_
  122.4 0.4 shard_map.61
  122.8 1.8 all-gather
  124.6 8.8 %all-gather.1 = f32[4,1,128]{2,1,0:T(1,128)S(1)} all-gather(f32[1,1,128]{2,1,0:T(1,128)S(1)} %fusion.3), channel_id=1, replica_groups=mesh['gx_0'=4,'gx_1'=2,'gy'=4,'gz_0'=8,'gz_1'=4] {'gy'}, dimensions={0}, use_global_device_ids=true | all-gather | bytes 2560 | tf_op jit(solution)/shard_map/all_gather | solution.py:507
  133.4 9.0 %all-gather.2 = f32[4,1,128]{2,1,0:T(1,128)S(1)} all-gather(f32[1,1,128]{2,1,0:T(1,128)S(1)} %fusion.2), channel_id=1, replica_groups=mesh['gx_0'=4,'gx_1'=2,'gy'=4,'gz_0'=8,'gz_1'=4] {'gz_1'}, dimensions={0}, use_global_device_ids=true | all-gather | bytes 2560 | tf_op jit(solution)/shard_map/all_gather | solution.py:507
  142.4 1.9 %collective-permute-start.18 = (f32[1,128]{1,0:T(1,128)S(1)}, f32[1,128]{1,0:T(1,128)S(1)}, u32[]{:S(2)}, u32[]{:S(2)}) collective-permute-start(f32[1,128]{1,0:T(1,128)S(1)} %bitcast_select_fusion.3), channel_id=1, source_target_pairs={{0,788},{1,793},{2,798},{3,3},{4,792},{5,797},{6,2},{7,7},{8,796},... | collective-permute-start | bytes 1544 | tf_op jit(solution)/shard_map/ppermute | solution.py:525
  144.4 0.6 copy.6
  145.0 3.8 %collective-permute-done.18 = f32[1,128]{1,0:T(1,128)S(1)} collective-permute-done((f32[1,128]{1,0:T(1,128)S(1)}, f32[1,128]{1,0:T(1,128)S(1)}, u32[]{:S(2)}, u32[]{:S(2)}) %collective-permute-start.18) | collective-permute-done | bytes 544 | tf_op jit(solution)/shard_map/ppermute | solution.py:525
  148.8 1.8 all-gather.3
  150.6 7.9 %all-gather.4 = f32[4,1,128]{2,1,0:T(1,128)S(1)} all-gather(f32[1,1,128]{2,1,0:T(1,128)S(1)} %fusion.1), channel_id=1, replica_groups=mesh['gx_0'=4,'gx_1'=2,'gy'=4,'gz_0'=8,'gz_1'=4] {'gz_1'}, dimensions={0}, use_global_device_ids=true | all-gather | bytes 2560 | tf_op jit(solution)/shard_map/all_gather | solution.py:507
  158.5 21.8 %all-gather.5 = f32[4,1,128]{2,1,0:T(1,128)S(1)} all-gather(f32[1,1,128]{2,1,0:T(1,128)S(1)} %fusion), channel_id=1, replica_groups=mesh['gx_0'=4,'gx_1'=2,'gy'=4,'gz_0'=8,'gz_1'=4] {'gx_0'}, dimensions={0}, use_global_device_ids=true | all-gather | bytes 2560 | tf_op jit(solution)/shard_map/all_gather | solution.py:507
  180.4 0.9 shard_map.62
  (12 shorter events, 0.2 us)
Async XLA Ops:
  1.7 49.3 %collective-permute-start = (f32[9,8,128]{2,1,0:T(8,128)S(1)}, f32[9,8,128]{2,1,0:T(8,128)S(1)}, u32[]{:S(2)}, u32[]{:S(2)}) collective-permute-start(f32[9,8,128]{2,1,0:T(8,128)S(1)} %get-tuple-element.39), channel_id=1, source_target_pairs={{0,896},{128,256},{256,128},{384,512},{512,384},{640,768},{768,640... | collective-permute-start | bytes 110600 | tf_op jit(solution)/shard_map/ppermute | solution.py:501
  24.1 26.9 %collective-permute-start.5 = (f32[9,8,128]{2,1,0:T(8,128)S(1)}, f32[9,8,128]{2,1,0:T(8,128)S(1)}, u32[]{:S(2)}, u32[]{:S(2)}) collective-permute-start(f32[9,8,128]{2,1,0:T(8,128)S(1)} %get-tuple-element.44), channel_id=1, source_target_pairs={{0,128},{128,0},{256,384},{384,256},{512,640},{640,512},{768,896},... | collective-permute-start | bytes 110600 | tf_op jit(solution)/shard_map/ppermute | solution.py:501
  26.0 25.0 %collective-permute-start.2 = (f32[9,4,128]{2,1,0:T(4,128)S(1)}, f32[9,4,128]{2,1,0:T(4,128)S(1)}, u32[]{:S(2)}, u32[]{:S(2)}) collective-permute-start(f32[9,4,128]{2,1,0:T(4,128)S(1)} %get-tuple-element.41), channel_id=1, source_target_pairs={{0,96},{32,64},{64,32},{96,0},{1,97},{33,65},{65,33},{97,1},{2,98}... | collective-permute-start | bytes 55304 | tf_op jit(solution)/shard_map/ppermute | solution.py:501
  30.7 20.3 %collective-permute-start.3 = (f32[9,4,128]{2,1,0:T(4,128)S(1)}, f32[9,4,128]{2,1,0:T(4,128)S(1)}, u32[]{:S(2)}, u32[]{:S(2)}) collective-permute-start(f32[9,4,128]{2,1,0:T(4,128)S(1)} %get-tuple-element.42), channel_id=1, source_target_pairs={{0,32},{32,0},{64,96},{96,64},{1,33},{33,1},{65,97},{97,65},{2,34}... | collective-permute-start | bytes 55304 | tf_op jit(solution)/shard_map/ppermute | solution.py:501
  32.9 5.5 %collective-permute-start.1 = (f32[8,128]{1,0:T(8,128)S(1)}, f32[8,128]{1,0:T(8,128)S(1)}, u32[]{:S(2)}, u32[]{:S(2)}) collective-permute-start(f32[8,128]{1,0:T(8,128)S(1)} %get-tuple-element.40), channel_id=1, source_target_pairs={{0,31},{1,2},{2,1},{3,4},{4,3},{5,6},{6,5},{7,8},{8,7},{9,10},{10,... | collective-permute-start | bytes 12296 | tf_op jit(solution)/shard_map/ppermute | solution.py:501
  38.4 12.6 %collective-permute-start.4 = (f32[8,128]{1,0:T(8,128)S(1)}, f32[8,128]{1,0:T(8,128)S(1)}, u32[]{:S(2)}, u32[]{:S(2)}) collective-permute-start(f32[8,128]{1,0:T(8,128)S(1)} %get-tuple-element.43), channel_id=1, source_target_pairs={{0,1},{1,0},{2,3},{3,2},{4,5},{5,4},{6,7},{7,6},{8,9},{9,8},{10,11... | collective-permute-start | bytes 12296 | tf_op jit(solution)/shard_map/ppermute | solution.py:501
  51.6 27.1 %collective-permute-start.11 = (f32[5,8,128]{2,1,0:T(8,128)S(1)}, f32[5,8,128]{2,1,0:T(8,128)S(1)}, u32[]{:S(2)}, u32[]{:S(2)}) collective-permute-start(f32[5,8,128]{2,1,0:T(8,128)S(1)} %get-tuple-element.52), channel_id=1, source_target_pairs={{0,128},{128,0},{256,384},{384,256},{512,640},{640,512},{768,896},... | collective-permute-start | bytes 61448 | tf_op jit(solution)/shard_map/ppermute | solution.py:501
  53.5 25.2 %collective-permute-start.6 = (f32[5,8,128]{2,1,0:T(8,128)S(1)}, f32[5,8,128]{2,1,0:T(8,128)S(1)}, u32[]{:S(2)}, u32[]{:S(2)}) collective-permute-start(f32[5,8,128]{2,1,0:T(8,128)S(1)} %get-tuple-element.47), channel_id=1, source_target_pairs={{0,896},{128,256},{256,128},{384,512},{512,384},{640,768},{768,640... | collective-permute-start | bytes 61448 | tf_op jit(solution)/shard_map/ppermute | solution.py:501
  62.0 16.6 %collective-permute-start.8 = (f32[5,4,128]{2,1,0:T(4,128)S(1)}, f32[5,4,128]{2,1,0:T(4,128)S(1)}, u32[]{:S(2)}, u32[]{:S(2)}) collective-permute-start(f32[5,4,128]{2,1,0:T(4,128)S(1)} %get-tuple-element.49), channel_id=1, source_target_pairs={{0,96},{32,64},{64,32},{96,0},{1,97},{33,65},{65,33},{97,1},{2,98}... | collective-permute-start | bytes 30728 | tf_op jit(solution)/shard_map/ppermute | solution.py:501
  65.1 13.6 %collective-permute-start.9 = (f32[5,4,128]{2,1,0:T(4,128)S(1)}, f32[5,4,128]{2,1,0:T(4,128)S(1)}, u32[]{:S(2)}, u32[]{:S(2)}) collective-permute-start(f32[5,4,128]{2,1,0:T(4,128)S(1)} %get-tuple-element.50), channel_id=1, source_target_pairs={{0,32},{32,0},{64,96},{96,64},{1,33},{33,1},{65,97},{97,65},{2,34}... | collective-permute-start | bytes 30728 | tf_op jit(solution)/shard_map/ppermute | solution.py:501
  67.7 5.5 %collective-permute-start.10 = (f32[8,128]{1,0:T(8,128)S(1)}, f32[8,128]{1,0:T(8,128)S(1)}, u32[]{:S(2)}, u32[]{:S(2)}) collective-permute-start(f32[8,128]{1,0:T(8,128)S(1)} %get-tuple-element.51), channel_id=1, source_target_pairs={{0,1},{1,0},{2,3},{3,2},{4,5},{5,4},{6,7},{7,6},{8,9},{9,8},{10,11... | collective-permute-start | bytes 12296 | tf_op jit(solution)/shard_map/ppermute | solution.py:501
  73.2 5.5 %collective-permute-start.7 = (f32[8,128]{1,0:T(8,128)S(1)}, f32[8,128]{1,0:T(8,128)S(1)}, u32[]{:S(2)}, u32[]{:S(2)}) collective-permute-start(f32[8,128]{1,0:T(8,128)S(1)} %get-tuple-element.48), channel_id=1, source_target_pairs={{0,31},{1,2},{2,1},{3,4},{4,3},{5,6},{6,5},{7,8},{8,7},{9,10},{10,... | collective-permute-start | bytes 12296 | tf_op jit(solution)/shard_map/ppermute | solution.py:501
  79.0 43.4 %collective-permute-start.12 = (f32[8,8,128]{2,1,0:T(8,128)S(1)}, f32[8,8,128]{2,1,0:T(8,128)S(1)}, u32[]{:S(2)}, u32[]{:S(2)}) collective-permute-start(f32[8,8,128]{2,1,0:T(8,128)S(1)} %get-tuple-element.55), channel_id=1, source_target_pairs={{0,896},{128,256},{256,128},{384,512},{512,384},{640,768},{768,640... | collective-permute-start | bytes 98312 | tf_op jit(solution)/shard_map/ppermute | solution.py:501
  82.5 39.9 %collective-permute-start.17 = (f32[8,8,128]{2,1,0:T(8,128)S(1)}, f32[8,8,128]{2,1,0:T(8,128)S(1)}, u32[]{:S(2)}, u32[]{:S(2)}) collective-permute-start(f32[8,8,128]{2,1,0:T(8,128)S(1)} %get-tuple-element.60), channel_id=1, source_target_pairs={{0,128},{128,0},{256,384},{384,256},{512,640},{640,512},{768,896},... | collective-permute-start | bytes 98312 | tf_op jit(solution)/shard_map/ppermute | solution.py:501
  87.2 35.2 %collective-permute-start.14 = (f32[8,4,128]{2,1,0:T(4,128)S(1)}, f32[8,4,128]{2,1,0:T(4,128)S(1)}, u32[]{:S(2)}, u32[]{:S(2)}) collective-permute-start(f32[8,4,128]{2,1,0:T(4,128)S(1)} %get-tuple-element.57), channel_id=1, source_target_pairs={{0,96},{32,64},{64,32},{96,0},{1,97},{33,65},{65,33},{97,1},{2,98}... | collective-permute-start | bytes 49160 | tf_op jit(solution)/shard_map/ppermute | solution.py:501
  91.7 30.7 %collective-permute-start.15 = (f32[8,4,128]{2,1,0:T(4,128)S(1)}, f32[8,4,128]{2,1,0:T(4,128)S(1)}, u32[]{:S(2)}, u32[]{:S(2)}) collective-permute-start(f32[8,4,128]{2,1,0:T(4,128)S(1)} %get-tuple-element.58), channel_id=1, source_target_pairs={{0,32},{32,0},{64,96},{96,64},{1,33},{33,1},{65,97},{97,65},{2,34}... | collective-permute-start | bytes 49160 | tf_op jit(solution)/shard_map/ppermute | solution.py:501
  93.8 5.5 %collective-permute-start.13 = (f32[8,128]{1,0:T(8,128)S(1)}, f32[8,128]{1,0:T(8,128)S(1)}, u32[]{:S(2)}, u32[]{:S(2)}) collective-permute-start(f32[8,128]{1,0:T(8,128)S(1)} %get-tuple-element.56), channel_id=1, source_target_pairs={{0,31},{1,2},{2,1},{3,4},{4,3},{5,6},{6,5},{7,8},{8,7},{9,10},{10,... | collective-permute-start | bytes 12296 | tf_op jit(solution)/shard_map/ppermute | solution.py:501
  99.3 23.0 %collective-permute-start.16 = (f32[8,128]{1,0:T(8,128)S(1)}, f32[8,128]{1,0:T(8,128)S(1)}, u32[]{:S(2)}, u32[]{:S(2)}) collective-permute-start(f32[8,128]{1,0:T(8,128)S(1)} %get-tuple-element.59), channel_id=1, source_target_pairs={{0,1},{1,0},{2,3},{3,2},{4,5},{5,4},{6,7},{7,6},{8,9},{9,8},{10,11... | collective-permute-start | bytes 12296 | tf_op jit(solution)/shard_map/ppermute | solution.py:501
  142.4 6.4 %collective-permute-start.18 = (f32[1,128]{1,0:T(1,128)S(1)}, f32[1,128]{1,0:T(1,128)S(1)}, u32[]{:S(2)}, u32[]{:S(2)}) collective-permute-start(f32[1,128]{1,0:T(1,128)S(1)} %bitcast_select_fusion.3), channel_id=1, source_target_pairs={{0,788},{1,793},{2,798},{3,3},{4,792},{5,797},{6,2},{7,7},{8,796},... | collective-permute-start | bytes 1544 | tf_op jit(solution)/shard_map/ppermute | solution.py:525
